TPU v7x, 32 devices: a whole 2x2x4 slice. The times are simulated.
32 devices in a mesh: dp: 8 (over y, x, core), expert: 4 (over z).
Axes of the slice: x: 2, y: 2, z: 4, core: 2. Of those that a mesh axis runs over, the one named last changes fastest.
Arguments:
- hidden_states: bfloat16 [4, 8192, 4096], P(None, ('dp', 'expert')), may hold values from -8 to 8
- router_weight: bfloat16 [4, 8, 4096], replicated, may hold values from -0.125 to 0.125
- expert_ids: int32 [4, 8192, 2], P(None, ('dp', 'expert')), may hold values from 0 to 7, as said below
Outputs:
- router_grad: float32 [4, 8, 4096], P(None, None, 'dp')
- losses: float32 [4, 2], replicated
Inputs may be any that keep to these rules, and one draw needn't show every extreme that they name: `expert_ids`: each token names 2 different experts in each layer.
All inputs are finite; a program needn't handle non-finite values.
Results may differ from a plain program's by a relative error of at most 0.0018.
Values sent between devices are 32-bit elements; how exact they have to be, the bound alone decides.
A program may use at most 64 MiB of HBM per device.

v0:
```python
import jax
import jax.numpy as jnp
from jax import lax
from jax.sharding import PartitionSpec as P

balance_coef = 0.02
zloss_coef = 0.001


def local_counts(chosen, experts):
    labels = jnp.arange(experts, dtype=jnp.int32)[:, None]
    counts = jnp.zeros((experts,), jnp.float32)
    for slot in range(chosen.shape[1]):
        counts = counts + jnp.sum((chosen[:, slot][None, :] == labels).astype(jnp.float32), axis=1)
    return counts


def on_device(hidden_states, router_weight, expert_ids):
    layers = hidden_states.shape[0]
    rows = hidden_states.shape[1]
    experts = router_weight.shape[1]
    picks = expert_ids.shape[2]
    tokens_all = rows * lax.axis_size("dp") * lax.axis_size("expert")
    terms = []
    count_list = []
    prob_sums = []
    square_sums = []
    for layer in range(layers):
        states = hidden_states[layer]
        logits = lax.dot_general(
            router_weight[layer],
            states,
            (((1,), (1,)), ((), ())),
            preferred_element_type=jnp.float32,
        )
        expo = jnp.exp(logits)
        total = jnp.sum(expo, axis=0)
        probs = expo / total[None, :]
        lse = jnp.log(total)
        prob_sums.append(jnp.sum(probs, axis=1))
        square_sums.append(jnp.sum(lse * lse))
        counts = lax.psum(local_counts(expert_ids[layer], experts), ("dp", "expert"))
        count_list.append(counts)
        share = counts / (tokens_all * picks)
        pull = balance_coef * experts * share
        mixed = jnp.sum(probs * pull[:, None], axis=0)
        dlogits = probs * (pull[:, None] - mixed[None, :]) + 2.0 * zloss_coef * lse[None, :] * probs
        dlogits = dlogits.astype(jnp.bfloat16)
        term = jnp.dot(dlogits, states, preferred_element_type=jnp.float32)
        terms.append(term)
    columns = lax.psum_scatter(jnp.stack(terms), "dp", scatter_dimension=2, tiled=True)
    router_grad = lax.psum(columns, "expert")
    prob_total, square_total = lax.psum(
        (jnp.stack(prob_sums), jnp.stack(square_sums)), ("dp", "expert")
    )
    share_table = jnp.stack(count_list) / (tokens_all * picks)
    balance = experts * jnp.sum(share_table * prob_total / tokens_all, axis=1)
    zloss = square_total / tokens_all
    return (router_grad, jnp.stack([balance, zloss], axis=-1))


def solution(mesh):
    in_specs = (P(None, ("dp", "expert"), None), P(), P(None, ("dp", "expert"), None))
    out_specs = (P(None, None, "dp"), P())
    return jax.shard_map(
        on_device, mesh=mesh, in_specs=in_specs, out_specs=out_specs, check_vma=False
    )
```

profile of v0, /device:TPU:0, one launch (start us, length us, event | category | flops | bytes accessed | tf_op | source)
XLA Modules:
  0.0 158.2 jit_solution(140643967143512886)
XLA Ops:
  7.2 2.3 %fusion.65 = (f32[256]{0:T(256)S(1)}, f32[8,256]{1,0:T(8,128)S(1)}) fusion(bf16[4,256,4096]{2,1,0:T(8,128)(2,1)} %param.3, bf16[4,8,4096]{2,1,0:T(8,128)(2,1)} %param.4), kind=kOutput, calls=%fused_computation.112 | convolution fusion | flops 16779008 | bytes 2171904 | tf_op jit(solution)/shard_map/dot_general | solution.py:30
  9.5 2.3 %fusion.66 = (f32[256]{0:T(256)S(1)}, f32[8,256]{1,0:T(8,128)S(1)}) fusion(bf16[4,256,4096]{2,1,0:T(8,128)(2,1)} %param.3, bf16[4,8,4096]{2,1,0:T(8,128)(2,1)} %param.4), kind=kOutput, calls=%fused_computation.113 | convolution fusion | flops 16779008 | bytes 2171904 | tf_op jit(solution)/shard_map/dot_general | solution.py:30
  11.8 2.3 %fusion.63 = (f32[256]{0:T(256)S(1)}, f32[8,256]{1,0:T(8,128)S(1)}) fusion(bf16[4,256,4096]{2,1,0:T(8,128)(2,1)} %param.3, bf16[4,8,4096]{2,1,0:T(8,128)(2,1)} %param.4), kind=kOutput, calls=%fused_computation.110 | convolution fusion | flops 16779008 | bytes 2171904 | tf_op jit(solution)/shard_map/dot_general | solution.py:30
  14.1 0.7 slice_bitcast_fusion.3
  14.9 0.1 convert_reduce_fusion.6
  15.0 0.1 convert_reduce_fusion.7
  15.1 0.1 convert_reduce_fusion.4
  15.2 0.1 convert_reduce_fusion.5
  15.4 0.1 convert_reduce_fusion
  15.5 0.1 convert_reduce_fusion.1
  15.6 0.1 convert_reduce_fusion.2
  15.7 0.1 convert_reduce_fusion.3
  15.9 2.3 %fusion.64 = (f32[256]{0:T(256)S(1)}, f32[8,256]{1,0:T(8,128)S(1)}) fusion(bf16[4,256,4096]{2,1,0:T(8,128)(2,1)} %param.3, bf16[4,8,4096]{2,1,0:T(8,128)(2,1)} %param.4), kind=kOutput, calls=%fused_computation.111 | convolution fusion | flops 16779008 | bytes 2171904 | tf_op jit(solution)/shard_map/dot_general | solution.py:30
  18.2 42.0 %all-reduce.1 = (f32[8]{0:T(128)S(1)}, f32[8]{0:T(128)S(1)}, f32[8]{0:T(128)S(1)}, f32[8]{0:T(128)S(1)}) all-reduce(f32[8]{0:T(128)S(1)} %add.46, f32[8]{0:T(128)S(1)} %add.44, f32[8]{0:T(128)S(1)} %add.42, f32[8]{0:T(128)S(1)} %add.40), channel_id=1, replica_groups=mesh['dp'=8,'expert'=4] {'dp','expert'}, use_global_device_ids=true, to_apply=%region_18.0 | all-reduce | flops 32 | bytes 256 | tf_op jit(solution)/shard_map/psum | solution.py:42
  60.2 0.6 multiply_reduce_fusion.6
  60.8 0.7 multiply_reduce_fusion.7
  61.5 0.6 multiply_reduce_fusion.4
  62.1 0.6 multiply_reduce_fusion.5
  62.7 0.2 fusion.55
  62.9 2.0 %convolution_bitcast_fusion.3 = f32[1,8,4096]{2,1,0:T(8,128)S(1)} fusion(bf16[4,256,4096]{2,1,0:T(8,128)(2,1)} %param.3, f32[256]{0:T(256)S(1)} %get-tuple-element.29, f32[256]{0:T(256)S(1)} %get-tuple-element.3, f32[8]{0:T(128)S(1)} %broadcast_multiply_fusion.3, f32[8,256]{1,0:T(8,128)S(1)} %get-tuple-element.43, f32[256]{0:T(256)S(1)} %get-tuple-element.42), kind=kOutput, calls=%fused_computation.3 | convolution fusion | flops 16787456 | bytes 2239520 | tf_op jit(solution)/shard_map/dot_general | solution.py:49
  64.9 2.0 %convolution_bitcast_fusion.2 = f32[1,8,4096]{2,1,0:T(8,128)S(1)} fusion(bf16[4,256,4096]{2,1,0:T(8,128)(2,1)} %param.3, f32[256]{0:T(256)S(1)} %get-tuple-element.31, f32[256]{0:T(256)S(1)} %get-tuple-element.44, f32[8]{0:T(128)S(1)} %broadcast_multiply_fusion.2, f32[8,256]{1,0:T(8,128)S(1)} %get-tuple-element.41, f32[256]{0:T(256)S(1)} %get-tuple-element.40), kind=kOutput, calls=%fused_computation.2 | convolution fusion | flops 16787456 | bytes 2239520 | tf_op jit(solution)/shard_map/dot_general | solution.py:49
  66.9 0.2 fusion.57
  67.1 2.0 %convolution_bitcast_fusion.1 = f32[1,8,4096]{2,1,0:T(8,128)S(1)} fusion(bf16[4,256,4096]{2,1,0:T(8,128)(2,1)} %param.3, f32[256]{0:T(256)S(1)} %get-tuple-element.33, f32[256]{0:T(256)S(1)} %get-tuple-element.7, f32[8]{0:T(128)S(1)} %broadcast_multiply_fusion.1, f32[8,256]{1,0:T(8,128)S(1)} %get-tuple-element.39, f32[256]{0:T(256)S(1)} %get-tuple-element.38), kind=kOutput, calls=%fused_computation.1 | convolution fusion | flops 16787456 | bytes 2239520 | tf_op jit(solution)/shard_map/dot_general | solution.py:49
  69.1 2.0 %convolution_bitcast_fusion = f32[1,8,4096]{2,1,0:T(8,128)S(1)} fusion(bf16[4,256,4096]{2,1,0:T(8,128)(2,1)} %param.3, f32[256]{0:T(256)S(1)} %get-tuple-element.35, f32[256]{0:T(256)S(1)} %get-tuple-element.46, f32[8]{0:T(128)S(1)} %broadcast_multiply_fusion, f32[8,256]{1,0:T(8,128)S(1)} %get-tuple-element.37, f32[256]{0:T(256)S(1)} %get-tuple-element.36), kind=kOutput, calls=%fused_computation | convolution fusion | flops 16787456 | bytes 2239520 | tf_op jit(solution)/shard_map/dot_general | solution.py:49
  71.1 0.8 pad_maximum_fusion
  71.9 0.0 all-reduce.4.cloned.1.call-start
  72.0 2.6 %pad_maximum_fusion.3 = f32[4]{0:T(128)S(1)} fusion(f32[1]{0:T(128)} %bitcast.36, f32[1]{0:T(128)} %bitcast.35, f32[1]{0:T(128)} %bitcast.34, f32[1]{0:T(128)} %bitcast.33), kind=kLoop, calls=%fused_computation.95 | loop fusion | flops 12 | bytes 32 | tf_op jit(solution)/shard_map/stack | solution.py:54
  74.6 40.0 %all-reduce = (f32[4]{0:T(128)S(1)}, f32[4,8]{1,0:T(4,128)S(1)}) all-reduce(f32[4]{0:T(128)S(1)} %pad_maximum_fusion.3, f32[4,8]{1,0:T(4,128)S(1)} %pad_maximum_fusion.1), channel_id=1, replica_groups=mesh['dp'=8,'expert'=4] {'dp','expert'}, use_global_device_ids=true, to_apply=%region_32.0 | all-reduce | flops 36 | bytes 288 | tf_op jit(solution)/shard_map/psum | solution.py:53
  114.7 0.1 fusion.54
  114.8 0.6 pad_maximum_fusion.2
  115.4 34.5 %all-reduce.4.cloned.1.call-done = f32[4,8,512]{2,1,0:T(8,128)} async-done(((f32[4,8,512]{2,1,0:T(8,128)}), f32[4,8,512]{2,1,0:T(8,128)}) %all-reduce.4.cloned.1.call-update) | async-done | bytes 65552 | tf_op jit(solution)/shard_map/psum | solution.py:52
  149.9 1.5 copy.6
  (19 shorter events, 0.2 us)
Async XLA Ops:
  7.2 107.6 %reduce-scatter.2.cloned.1.call-start = ((), (), s32[]{:S(2)}) async-start(), calls=%async_computation.1 | async-start | bytes 589824 | tf_op jit(solution)/shard_map/reduce_scatter | solution.py:51
  71.9 78.0 %all-reduce.4.cloned.1.call-start = ((), (), s32[]{:S(2)}) async-start(), calls=%async_computation.2 | async-start | bytes 131072 | tf_op jit(solution)/shard_map/psum | solution.py:52
Sparse Core Ops, SparseCore 0:
  72.1 33.9 reduce-scatter.1
  115.0 34.9 all-reduce.3
where the time goes:
time: 159 us; the launch traced here: 158 us
  blocking collectives  82.1 us (52%)
  waiting for transfers between devices  34.6 us (22%)
  matrix products  17.3 us (11%)
  between operations  14.2 us (9%)
  other arithmetic  7.88 us (5%)
  local copies, waits for them, and re-layouts  2.23 us (1%)
    psum x1, blocking collectives, on_device(): lax.psum(local_counts(expert_ids[layer], experts), ('dp', 'expert'))  42 us
    psum x1, blocking collectives, on_device(): lax.psum((jnp.stack(prob_sums), jnp.stack(square_sums)), ('dp', 'expert'))  40 us
    psum x1, waiting for transfers between devices, on_device(): router_grad = lax.psum(columns, 'expert')  34.5 us
    dot_general x4, matrix products, on_device(): lax.dot_general(router_weight[layer], states, (((1,), (1,)), ((), ())), p...  9.21 us
    dot_general x4, matrix products, on_device(): term = jnp.dot(dlogits, states, preferred_element_type=jnp.float32)  8.06 us
  transfers between devices with their start and end apart: 2, of which 1 were waited for; matrix products, arithmetic and copies ran while one was open for 2% of the time, Pallas kernels for 0%

commit v1 on v0

v1 whole, which is shorter than its diff:
```python
import functools

import jax
import jax.numpy as jnp
from jax import lax
from jax.experimental import pallas as pl
from jax.experimental.pallas import tpu as pltpu
from jax.sharding import PartitionSpec as P

balance_coef = 0.02
zloss_coef = 0.001
MESH = pl.DeviceIdType.MESH


def kernel(
    nd, nz, tokens_all,
    x_hbm, w_hbm, ids_hbm, grad_ref, loss_ref,
    x, w, ids, term, recv, zbuf, cnt_d, cnt_z, st_d, st_z,
    x_sem, w_sem, ids_sem, cd_s, cd_r, cz_s, cz_r, sd_s, sd_r, sz_s, sz_r, td_s, td_r, tz_s, tz_r,
):
    layers, rows, _ = x.shape
    experts = w.shape[1]
    picks = ids.shape[1]
    width = term.shape[3]
    me_d = lax.axis_index("dp")
    me_z = lax.axis_index("expert")
    peers_d = [(k, lax.rem(me_d + k, nd)) for k in range(1, nd)]
    peers_z = [(k, lax.rem(me_z + k, nz)) for k in range(1, nz)]

    barrier = pltpu.get_barrier_semaphore()
    for _, peer in peers_z:
        pl.semaphore_signal(barrier, inc=1, device_id={"expert": peer}, device_id_type=MESH)
    for _, peer in peers_d:
        pl.semaphore_signal(barrier, inc=1, device_id={"dp": peer}, device_id_type=MESH)

    ids_copy = pltpu.make_async_copy(ids_hbm, ids, ids_sem)
    ids_copy.start()
    w_copy = pltpu.make_async_copy(w_hbm, w, w_sem)
    w_copy.start()
    pieces = 4 if rows % 64 == 0 else 1
    step = rows // pieces
    for layer in range(layers):
        for piece in range(pieces):
            part = pl.ds(piece * step, step)
            pltpu.make_async_copy(x_hbm.at[layer, part], x.at[layer, part], x_sem.at[layer]).start()

    def exchange(axis, peers, buf, me, send_sem, recv_sem):
        copies = []
        for k, peer in peers:
            copy = pltpu.make_async_remote_copy(
                src_ref=buf.at[me],
                dst_ref=buf.at[me],
                send_sem=send_sem.at[k - 1],
                recv_sem=recv_sem,
                device_id={axis: peer},
                device_id_type=MESH,
            )
            copy.start()
            copies.append(copy)
        return copies

    def arrived(buf, count, sem):
        part = buf.at[pl.ds(0, count)]
        pltpu.make_async_copy(part, part, sem).wait()

    def total_of(buf, count):
        out = buf[0]
        for i in range(1, count):
            out = out + buf[i]
        return out

    labels = lax.broadcasted_iota(jnp.int32, (experts, rows), 0)
    lane = lax.broadcasted_iota(jnp.int32, cnt_d.shape[1:], 1)
    ids_copy.wait()
    counts = jnp.zeros(cnt_d.shape[1:], jnp.float32)
    for layer in range(layers):
        hits = jnp.zeros((experts, rows), jnp.float32)
        for slot in range(picks):
            chosen = ids[layer, pl.ds(slot, 1), :]
            hits = hits + (jnp.broadcast_to(chosen, labels.shape) == labels).astype(jnp.float32)
        counts = jnp.where(lane == layer, jnp.sum(hits, axis=1, keepdims=True), counts)
    cnt_d[me_d] = counts

    probs, lses = [], []

    def forward(layer):
        pltpu.make_async_copy(x_hbm.at[layer], x.at[layer], x_sem.at[layer]).wait()
        logits = lax.dot_general(
            w[layer], x[layer], (((1,), (1,)), ((), ())), preferred_element_type=jnp.float32
        )
        expo = jnp.exp(logits)
        total = jnp.sum(expo, axis=0, keepdims=True)
        probs.append(expo / total)
        lses.append(jnp.log(total))

    w_copy.wait()
    pending = []
    wait_at = max(layers - 2, 0)
    for layer in range(layers):
        forward(layer)
        if layer == 0:
            pl.semaphore_wait(barrier, nd + nz - 2)
            pending += exchange("dp", peers_d, cnt_d, me_d, cd_s, cd_r)
        if layer == wait_at:
            arrived(cnt_d, nd - 1, cd_r)
            cnt_z[me_z] = total_of(cnt_d, nd)
            pending += exchange("expert", peers_z, cnt_z, me_z, cz_s, cz_r)
    arrived(cnt_z, nz - 1, cz_r)
    share = total_of(cnt_z, nz) / (tokens_all * picks)

    def combine(layer):
        arrived(recv.at[layer], nd - 1, td_r.at[layer])
        out = term[layer, me_d]
        for k in range(nd - 1):
            out = out + recv[layer, k]
        zbuf[layer, me_z] = out
        return exchange("expert", peers_z, zbuf.at[layer], me_z, tz_s.at[layer], tz_r.at[layer])

    row = lax.broadcasted_iota(jnp.int32, cnt_d.shape[1:], 0)
    stats = jnp.zeros(cnt_d.shape[1:], jnp.float32)
    for layer in range(layers):
        share_l = share[:, layer:layer + 1]
        pull = balance_coef * experts * share_l
        mixed = jnp.sum(probs[layer] * pull, axis=0, keepdims=True)
        dlogits = probs[layer] * (pull - mixed) + 2.0 * zloss_coef * lses[layer] * probs[layer]
        dlogits = dlogits.astype(jnp.bfloat16)
        for d in range(nd):
            term[layer, d] = jnp.dot(
                dlogits, x[layer, :, d * width:(d + 1) * width], preferred_element_type=jnp.float32
            )
        for k, peer in peers_d:
            copy = pltpu.make_async_remote_copy(
                src_ref=term.at[layer, peer],
                dst_ref=recv.at[layer, k - 1],
                send_sem=td_s.at[layer, k - 1],
                recv_sem=td_r.at[layer],
                device_id={"dp": peer},
                device_id_type=MESH,
            )
            copy.start()
            pending.append(copy)
        prob_sum = jnp.sum(probs[layer], axis=1, keepdims=True)
        balance = experts * jnp.sum(share_l * prob_sum / tokens_all, axis=0, keepdims=True)
        zloss = jnp.sum(lses[layer] * lses[layer], axis=1, keepdims=True) / tokens_all
        stats = jnp.where((row == layer) & (lane == 0), balance, stats)
        stats = jnp.where((row == layer) & (lane == 1), zloss, stats)
        if layer >= 2:
            pending += combine(layer - 2)
    st_d[me_d] = stats
    pending += exchange("dp", peers_d, st_d, me_d, sd_s, sd_r)
    for layer in range(max(layers - 2, 0), layers):
        pending += combine(layer)
    arrived(st_d, nd - 1, sd_r)
    st_z[me_z] = total_of(st_d, nd)
    pending += exchange("expert", peers_z, st_z, me_z, sz_s, sz_r)
    for layer in range(layers):
        arrived(zbuf.at[layer], nz - 1, tz_r.at[layer])
        grad_ref[layer] = total_of(zbuf.at[layer], nz)
    arrived(st_z, nz - 1, sz_r)
    loss_ref[...] = total_of(st_z, nz)
    for copy in pending:
        copy.wait_send()


def on_device(nd, nz, hidden_states, router_weight, expert_ids):
    layers, rows, depth = hidden_states.shape
    experts = router_weight.shape[1]
    picks = expert_ids.shape[2]
    width = depth // nd
    tokens_all = rows * nd * nz
    tile = (max(8, experts, layers), 128)
    dma = pltpu.SemaphoreType.DMA
    anywhere = pl.BlockSpec(memory_space=pl.ANY)
    inside = pl.BlockSpec(memory_space=pltpu.VMEM)
    grad, loss = pl.pallas_call(
        functools.partial(kernel, nd, nz, tokens_all),
        out_shape=(
            jax.ShapeDtypeStruct((layers, experts, width), jnp.float32),
            jax.ShapeDtypeStruct(tile, jnp.float32),
        ),
        in_specs=[anywhere] * 3,
        out_specs=(inside, inside),
        scratch_shapes=[
            pltpu.VMEM(hidden_states.shape, jnp.bfloat16),
            pltpu.VMEM(router_weight.shape, jnp.bfloat16),
            pltpu.VMEM((layers, picks, rows), jnp.int32),
            pltpu.VMEM((layers, nd, experts, width), jnp.float32),
            pltpu.VMEM((layers, nd - 1, experts, width), jnp.float32),
            pltpu.VMEM((layers, nz, experts, width), jnp.float32),
            pltpu.VMEM((nd,) + tile, jnp.float32),
            pltpu.VMEM((nz,) + tile, jnp.float32),
            pltpu.VMEM((nd,) + tile, jnp.float32),
            pltpu.VMEM((nz,) + tile, jnp.float32),
            dma((layers,)), dma, dma,
            dma((nd - 1,)), dma, dma((nz - 1,)), dma,
            dma((nd - 1,)), dma, dma((nz - 1,)), dma,
            dma((layers, nd - 1)), dma((layers,)), dma((layers, nz - 1)), dma((layers,)),
        ],
        compiler_params=pltpu.CompilerParams(collective_id=0, has_side_effects=True),
    )(hidden_states, router_weight, jnp.transpose(expert_ids, (0, 2, 1)))
    return grad, loss[:layers, :2]


def solution(mesh):
    in_specs = (P(None, ("dp", "expert"), None), P(), P(None, ("dp", "expert"), None))
    out_specs = (P(None, None, "dp"), P())
    return jax.shard_map(
        functools.partial(on_device, mesh.shape["dp"], mesh.shape["expert"]),
        mesh=mesh, in_specs=in_specs, out_specs=out_specs, check_vma=False,
    )
```

time: 159 us -> 32 us (0.20)
  blocking collectives: 82.1 us -> 0 us
  waiting for transfers between devices: 34.6 us -> 0 us
  Pallas kernels: 0 us -> 28.3 us
  matrix products: 17.3 us -> 0 us
  between operations: 14.2 us -> 0.64 us
  other arithmetic: 7.88 us -> 0 us
    psum x2 -> x0, blocking collectives: 82.1 us -> none  [the longest x1 42 us: on_device(): lax.psum(local_counts(expert_ids[layer], experts), ('dp', 'expert'))]
    psum x1 -> x0, waiting for transfers between devices: 34.5 us -> none  [on_device(): router_grad = lax.psum(columns, 'expert')]
    pallas_call x0 -> x1, Pallas kernels: none -> 28.3 us  [on_device(): pl.pallas_call(functools.partial(kernel, nd, nz, tokens_all), out_shape=(...]
    dot_general x8 -> x0, matrix products: 17.3 us -> none  [the longest x4 9.21 us: on_device(): lax.dot_general(router_weight[layer], states, (((1,), (1,)), ((), ())), p...]
    another operation x5 -> x0, other arithmetic: 4.01 us -> none  [the longest x1 2.6 us: on_device(): jnp.stack(square_sums)]
    reduce_sum x15 -> x0, other arithmetic: 3.84 us -> none  [the longest x4 2.48 us: on_device(): square_sums.append(jnp.sum(lse * lse))]
  transfers between devices with their start and end apart: 2 -> 0, of which waited for: 1 -> 0; matrix products, arithmetic and copies ran while one was open for 2% -> 0% of each run, Pallas kernels for 0% -> 0%
where the time goes in v1:
time: 32 us; the launch traced here: 31.8 us
  Pallas kernels  28.3 us (88%)
  local copies, waits for them, and re-layouts  2.8 us (9%)
  between operations  0.64 us (2%)
    pallas_call x1, Pallas kernels, on_device(): pl.pallas_call(functools.partial(kernel, nd, nz, tokens_all), out_shape=(...  28.3 us
    unnamed x2, local copies, waits for them, and re-layouts  2.12 us
    slice x1, local copies, waits for them, and re-layouts, on_device(): return (grad, loss[:layers, :2])  0.68 us

profile of v1, /device:TPU:0, one launch (start us, length us, event | category | flops | bytes accessed | tf_op | source)
XLA Modules:
  0.0 31.8 jit_solution(833084577981133468)
XLA Ops:
  0.6 28.3 %shard_map.50 = (f32[4,8,512]{2,1,0:T(8,128)}, f32[8,128]{1,0:T(8,128)}) custom-call(bf16[4,256,4096]{2,1,0:T(8,128)(2,1)} %x_hbm.1, bf16[4,8,4096]{2,1,0:T(8,128)(2,1)} %w_hbm.1, s32[4,2,256]{2,1,0:T(2,128)} %bitcast.1), custom_call_target="tpu_custom_call" | custom-call | tf_op jit(solution)/shard_map/pallas_call | solution.py:175
  29.0 0.7 %slice.3 = f32[4,2]{1,0:T(4,128)S(1)} slice(f32[8,128]{1,0:T(8,128)} %get-tuple-element.5), slice={[0:4], [0:2]} | slice | bytes 64 | tf_op jit(solution)/shard_map/slice | solution.py:201
  29.7 0.7 %copy.5 = f32[4,2]{0,1:T(2,128)} copy(f32[4,2]{1,0:T(4,128)S(1)} %slice.3) | data formatting | bytes 64
  30.3 1.5 %copy.7 = f32[4,8,512]{2,1,0:T(8,128)} copy(f32[4,8,512]{2,1,0:T(8,128)} %get-tuple-element.10) | data formatting | bytes 131072

commit v2 on v1

--- a/solution.py
+++ b/solution.py
@@ -15,16 +15,21 @@
 def kernel(
     nd, nz, tokens_all,
     x_hbm, w_hbm, ids_hbm, grad_ref, loss_ref,
-    x, w, ids, term, recv, zbuf, cnt_d, cnt_z, st_d, st_z,
-    x_sem, w_sem, ids_sem, cd_s, cd_r, cz_s, cz_r, sd_s, sd_r, sz_s, sz_r, td_s, td_r, tz_s, tz_r,
+    x, w, ids, term, half, part_sum, recv, zbuf, cnt_d, cnt_z, st_d, st_z,
+    x_sem, w_sem, ids_sem, cd_s, cd_r, cz_s, cz_r, sd_s, sd_r, sz_s, sz_r,
+    tp_s, tp_r, td_s, td_r, tz_s, tz_r,
 ):
     layers, rows, _ = x.shape
     experts = w.shape[1]
     picks = ids.shape[1]
-    width = term.shape[3]
+    width = term.shape[4]
+    chips = nd // 2
     me_d = lax.axis_index("dp")
     me_z = lax.axis_index("expert")
     peers_d = [(k, lax.rem(me_d + k, nd)) for k in range(1, nd)]
+    core, chip = lax.rem(me_d, 2), me_d // 2
+    partner = me_d + 1 - 2 * core
+    peers_c = [(k, lax.rem(chip + k, chips)) for k in range(1, chips)]
     peers_z = [(k, lax.rem(me_z + k, nz)) for k in range(1, nz)]
 
     barrier = pltpu.get_barrier_semaphore()
@@ -93,14 +98,12 @@
         probs.append(expo / total)
         lses.append(jnp.log(total))
 
+    pl.semaphore_wait(barrier, nd + nz - 2)
+    pending = exchange("dp", peers_d, cnt_d, me_d, cd_s, cd_r)
     w_copy.wait()
-    pending = []
-    wait_at = max(layers - 2, 0)
+    wait_at = min(1, layers - 1)
     for layer in range(layers):
         forward(layer)
-        if layer == 0:
-            pl.semaphore_wait(barrier, nd + nz - 2)
-            pending += exchange("dp", peers_d, cnt_d, me_d, cd_s, cd_r)
         if layer == wait_at:
             arrived(cnt_d, nd - 1, cd_r)
             cnt_z[me_z] = total_of(cnt_d, nd)
@@ -108,56 +111,79 @@
     arrived(cnt_z, nz - 1, cz_r)
     share = total_of(cnt_z, nz) / (tokens_all * picks)
 
-    def combine(layer):
-        arrived(recv.at[layer], nd - 1, td_r.at[layer])
-        out = term[layer, me_d]
-        for k in range(nd - 1):
-            out = out + recv[layer, k]
-        zbuf[layer, me_z] = out
-        return exchange("expert", peers_z, zbuf.at[layer], me_z, tz_s.at[layer], tz_r.at[layer])
-
-    row = lax.broadcasted_iota(jnp.int32, cnt_d.shape[1:], 0)
-    stats = jnp.zeros(cnt_d.shape[1:], jnp.float32)
-    for layer in range(layers):
-        share_l = share[:, layer:layer + 1]
-        pull = balance_coef * experts * share_l
+    def half_term(layer, dlogits, parity):
+        for c in range(chips):
+            at = (2 * c + parity) * width
+            at = pl.multiple_of(at, 128)
+            term[layer, parity, c] = jnp.dot(
+                dlogits, x[layer, :, pl.ds(at, width)], preferred_element_type=jnp.float32
+            )
+
+    to_partner = []
+    for layer in range(layers):
+        pull = balance_coef * experts * share[:, layer:layer + 1]
         mixed = jnp.sum(probs[layer] * pull, axis=0, keepdims=True)
         dlogits = probs[layer] * (pull - mixed) + 2.0 * zloss_coef * lses[layer] * probs[layer]
         dlogits = dlogits.astype(jnp.bfloat16)
-        for d in range(nd):
-            term[layer, d] = jnp.dot(
-                dlogits, x[layer, :, d * width:(d + 1) * width], preferred_element_type=jnp.float32
-            )
-        for k, peer in peers_d:
+        half_term(layer, dlogits, 1 - core)
+        copy = pltpu.make_async_remote_copy(
+            src_ref=term.at[layer, 1 - core],
+            dst_ref=half.at[layer],
+            send_sem=tp_s.at[layer],
+            recv_sem=tp_r.at[layer],
+            device_id={"dp": partner},
+            device_id_type=MESH,
+        )
+        copy.start()
+        to_partner.append(copy)
+        half_term(layer, dlogits, core)
+
+    for layer in range(layers):
+        to_partner[layer].wait_recv()
+        for c in range(chips):
+            part_sum[layer, c] = term[layer, core, c] + half[layer, c]
+        for k, peer in peers_c:
             copy = pltpu.make_async_remote_copy(
-                src_ref=term.at[layer, peer],
+                src_ref=part_sum.at[layer, peer],
                 dst_ref=recv.at[layer, k - 1],
                 send_sem=td_s.at[layer, k - 1],
                 recv_sem=td_r.at[layer],
-                device_id={"dp": peer},
+                device_id={"dp": 2 * peer + core},
                 device_id_type=MESH,
             )
             copy.start()
             pending.append(copy)
+    pending += to_partner
+
+    row = lax.broadcasted_iota(jnp.int32, cnt_d.shape[1:], 0)
+    stats = jnp.zeros(cnt_d.shape[1:], jnp.float32)
+    for layer in range(layers):
+        share_l = share[:, layer:layer + 1]
         prob_sum = jnp.sum(probs[layer], axis=1, keepdims=True)
         balance = experts * jnp.sum(share_l * prob_sum / tokens_all, axis=0, keepdims=True)
         zloss = jnp.sum(lses[layer] * lses[layer], axis=1, keepdims=True) / tokens_all
-        stats = jnp.where((row == layer) & (lane == 0), balance, stats)
-        stats = jnp.where((row == layer) & (lane == 1), zloss, stats)
-        if layer >= 2:
-            pending += combine(layer - 2)
+        stats = jnp.where((row == 0) & (lane == layer), balance, stats)
+        stats = jnp.where((row == 1) & (lane == layer), zloss, stats)
     st_d[me_d] = stats
     pending += exchange("dp", peers_d, st_d, me_d, sd_s, sd_r)
-    for layer in range(max(layers - 2, 0), layers):
-        pending += combine(layer)
-    arrived(st_d, nd - 1, sd_r)
-    st_z[me_z] = total_of(st_d, nd)
-    pending += exchange("expert", peers_z, st_z, me_z, sz_s, sz_r)
+    for layer in range(layers):
+        if layer == layers - 1:
+            arrived(st_d, nd - 1, sd_r)
+            st_z[me_z] = total_of(st_d, nd)
+            pending += exchange("expert", peers_z, st_z, me_z, sz_s, sz_r)
+        arrived(recv.at[layer], chips - 1, td_r.at[layer])
+        out = part_sum[layer, chip]
+        for k in range(chips - 1):
+            out = out + recv[layer, k]
+        zbuf[layer, me_z] = out
+        pending += exchange(
+            "expert", peers_z, zbuf.at[layer], me_z, tz_s.at[layer], tz_r.at[layer]
+        )
     for layer in range(layers):
         arrived(zbuf.at[layer], nz - 1, tz_r.at[layer])
         grad_ref[layer] = total_of(zbuf.at[layer], nz)
     arrived(st_z, nz - 1, sz_r)
-    loss_ref[...] = total_of(st_z, nz)
+    loss_ref[...] = total_of(st_z, nz)[:2, :layers]
     for copy in pending:
         copy.wait_send()
 
@@ -167,16 +193,17 @@
     experts = router_weight.shape[1]
     picks = expert_ids.shape[2]
     width = depth // nd
+    chips = nd // 2
     tokens_all = rows * nd * nz
-    tile = (max(8, experts, layers), 128)
+    tile = (max(8, experts), 128)
     dma = pltpu.SemaphoreType.DMA
     anywhere = pl.BlockSpec(memory_space=pl.ANY)
     inside = pl.BlockSpec(memory_space=pltpu.VMEM)
     grad, loss = pl.pallas_call(
         functools.partial(kernel, nd, nz, tokens_all),
         out_shape=(
-            jax.ShapeDtypeStruct((layers, experts, width), jnp.float32),
-            jax.ShapeDtypeStruct(tile, jnp.float32),
+            pltpu.VMEM((layers, experts, width), jnp.float32),
+            pltpu.VMEM((2, layers), jnp.float32),
         ),
         in_specs=[anywhere] * 3,
         out_specs=(inside, inside),
@@ -184,8 +211,10 @@
             pltpu.VMEM(hidden_states.shape, jnp.bfloat16),
             pltpu.VMEM(router_weight.shape, jnp.bfloat16),
             pltpu.VMEM((layers, picks, rows), jnp.int32),
-            pltpu.VMEM((layers, nd, experts, width), jnp.float32),
-            pltpu.VMEM((layers, nd - 1, experts, width), jnp.float32),
+            pltpu.VMEM((layers, 2, chips, experts, width), jnp.float32),
+            pltpu.VMEM((layers, chips, experts, width), jnp.float32),
+            pltpu.VMEM((layers, chips, experts, width), jnp.float32),
+            pltpu.VMEM((layers, chips - 1, experts, width), jnp.float32),
             pltpu.VMEM((layers, nz, experts, width), jnp.float32),
             pltpu.VMEM((nd,) + tile, jnp.float32),
             pltpu.VMEM((nz,) + tile, jnp.float32),
@@ -194,11 +223,12 @@
             dma((layers,)), dma, dma,
             dma((nd - 1,)), dma, dma((nz - 1,)), dma,
             dma((nd - 1,)), dma, dma((nz - 1,)), dma,
-            dma((layers, nd - 1)), dma((layers,)), dma((layers, nz - 1)), dma((layers,)),
+            dma((layers,)), dma((layers,)),
+            dma((layers, chips - 1)), dma((layers,)), dma((layers, nz - 1)), dma((layers,)),
         ],
         compiler_params=pltpu.CompilerParams(collective_id=0, has_side_effects=True),
     )(hidden_states, router_weight, jnp.transpose(expert_ids, (0, 2, 1)))
-    return grad, loss[:layers, :2]
+    return grad, jnp.transpose(loss)
 
 
 def solution(mesh):

time: 32 us -> 27.5 us (0.86)
  Pallas kernels: 28.3 us -> 25.5 us
  local copies, waits for them, and re-layouts: 2.8 us -> 1.19 us
    pallas_call x1, Pallas kernels: 28.3 us -> 25.5 us  [on_device(): pl.pallas_call(functools.partial(kernel, nd, nz, tokens_all), out_shape=(...]
    unnamed x2, local copies, waits for them, and re-layouts: 2.12 us -> 1.19 us
    slice x1 -> x0, local copies, waits for them, and re-layouts: 0.68 us -> none  [on_device(): return (grad, loss[:layers, :2])]
where the time goes in v2:
time: 27.5 us; the launch traced here: 27.4 us
  Pallas kernels  25.5 us (93%)
  local copies, waits for them, and re-layouts  1.19 us (4%)
  between operations  0.64 us (2%)
    pallas_call x1, Pallas kernels, on_device(): pl.pallas_call(functools.partial(kernel, nd, nz, tokens_all), out_shape=(...  25.5 us
    unnamed x2, local copies, waits for them, and re-layouts  1.19 us

profile of v2, /device:TPU:0, one launch (start us, length us, event | category | flops | bytes accessed | tf_op | source)
XLA Modules:
  0.0 27.4 jit_solution(14708135024038774867)
XLA Ops:
  0.6 25.5 %shard_map.50 = (f32[4,8,512]{2,1,0:T(8,128)S(1)}, f32[2,4]{1,0:T(2,128)S(1)}) custom-call(bf16[4,256,4096]{2,1,0:T(8,128)(2,1)} %x_hbm.1, bf16[4,8,4096]{2,1,0:T(8,128)(2,1)} %w_hbm.1, s32[4,2,256]{2,1,0:T(2,128)} %bitcast.3), custom_call_target="tpu_custom_call" | custom-call | tf_op jit(solution)/shard_map/pallas_call | solution.py:202
  26.2 0.6 %copy.7 = f32[4,8,512]{2,1,0:T(8,128)} copy(f32[4,8,512]{2,1,0:T(8,128)S(1)} %get-tuple-element.6) | data formatting | bytes 131072
  26.8 0.6 %copy.8 = f32[4,2]{0,1:T(2,128)} copy(f32[4,2]{0,1:T(2,128)S(1)} %bitcast.2) | data formatting | bytes 64

commit v3 on v2

--- a/solution.py
+++ b/solution.py
@@ -75,16 +75,18 @@
         return out
 
     labels = lax.broadcasted_iota(jnp.int32, (experts, rows), 0)
-    lane = lax.broadcasted_iota(jnp.int32, cnt_d.shape[1:], 1)
+    lanes = cnt_d.shape[2]
+    lane = lax.broadcasted_iota(jnp.int32, (experts, lanes), 1)
+    row = lax.broadcasted_iota(jnp.int32, (experts, lanes), 0)
     ids_copy.wait()
-    counts = jnp.zeros(cnt_d.shape[1:], jnp.float32)
+    counts = jnp.zeros((experts, lanes), jnp.float32)
     for layer in range(layers):
         hits = jnp.zeros((experts, rows), jnp.float32)
         for slot in range(picks):
             chosen = ids[layer, pl.ds(slot, 1), :]
             hits = hits + (jnp.broadcast_to(chosen, labels.shape) == labels).astype(jnp.float32)
-        counts = jnp.where(lane == layer, jnp.sum(hits, axis=1, keepdims=True), counts)
-    cnt_d[me_d] = counts
+        counts = jnp.where(lane == layer * experts + row, jnp.sum(hits, axis=1, keepdims=True), counts)
+    cnt_d[me_d] = jnp.sum(counts, axis=0, keepdims=True)
 
     probs, lses = [], []
 
@@ -109,7 +111,11 @@
             cnt_z[me_z] = total_of(cnt_d, nd)
             pending += exchange("expert", peers_z, cnt_z, me_z, cz_s, cz_r)
     arrived(cnt_z, nz - 1, cz_r)
-    share = total_of(cnt_z, nz) / (tokens_all * picks)
+    share_row = total_of(cnt_z, nz) / (tokens_all * picks)
+    shares = [
+        jnp.sum(jnp.where(lane == layer * experts + row, share_row, 0.0), axis=1, keepdims=True)
+        for layer in range(layers)
+    ]
 
     def half_term(layer, dlogits, parity):
         for c in range(chips):
@@ -121,7 +127,7 @@
 
     to_partner = []
     for layer in range(layers):
-        pull = balance_coef * experts * share[:, layer:layer + 1]
+        pull = balance_coef * experts * shares[layer]
         mixed = jnp.sum(probs[layer] * pull, axis=0, keepdims=True)
         dlogits = probs[layer] * (pull - mixed) + 2.0 * zloss_coef * lses[layer] * probs[layer]
         dlogits = dlogits.astype(jnp.bfloat16)
@@ -155,15 +161,14 @@
             pending.append(copy)
     pending += to_partner
 
-    row = lax.broadcasted_iota(jnp.int32, cnt_d.shape[1:], 0)
-    stats = jnp.zeros(cnt_d.shape[1:], jnp.float32)
-    for layer in range(layers):
-        share_l = share[:, layer:layer + 1]
+    line = lax.broadcasted_iota(jnp.int32, (1, lanes), 1)
+    stats = jnp.zeros((1, lanes), jnp.float32)
+    for layer in range(layers):
         prob_sum = jnp.sum(probs[layer], axis=1, keepdims=True)
-        balance = experts * jnp.sum(share_l * prob_sum / tokens_all, axis=0, keepdims=True)
+        balance = experts * jnp.sum(shares[layer] * prob_sum / tokens_all, axis=0, keepdims=True)
         zloss = jnp.sum(lses[layer] * lses[layer], axis=1, keepdims=True) / tokens_all
-        stats = jnp.where((row == 0) & (lane == layer), balance, stats)
-        stats = jnp.where((row == 1) & (lane == layer), zloss, stats)
+        stats = jnp.where(line == layer, balance, stats)
+        stats = jnp.where(line == layers + layer, zloss, stats)
     st_d[me_d] = stats
     pending += exchange("dp", peers_d, st_d, me_d, sd_s, sd_r)
     for layer in range(layers):
@@ -183,7 +188,9 @@
         arrived(zbuf.at[layer], nz - 1, tz_r.at[layer])
         grad_ref[layer] = total_of(zbuf.at[layer], nz)
     arrived(st_z, nz - 1, sz_r)
-    loss_ref[...] = total_of(st_z, nz)[:2, :layers]
+    losses = total_of(st_z, nz)
+    loss_ref[0:1] = losses[:, :layers]
+    loss_ref[1:2] = losses[:, layers:2 * layers]
     for copy in pending:
         copy.wait_send()
 
@@ -195,7 +202,7 @@
     width = depth // nd
     chips = nd // 2
     tokens_all = rows * nd * nz
-    tile = (max(8, experts), 128)
+    tile = (1, pl.cdiv(layers * experts, 128) * 128)
     dma = pltpu.SemaphoreType.DMA
     anywhere = pl.BlockSpec(memory_space=pl.ANY)
     inside = pl.BlockSpec(memory_space=pltpu.VMEM)

time: 27.5 us -> 27.2 us (0.989)
    pallas_call x1, Pallas kernels: 25.5 us -> 25.3 us  [on_device(): pl.pallas_call(functools.partial(kernel, nd, nz, tokens_all), out_shape=(...]
where the time goes in v3:
time: 27.2 us; the launch traced here: 27.1 us
  Pallas kernels  25.3 us (93%)
  local copies, waits for them, and re-layouts  1.19 us (4%)
  between operations  0.64 us (2%)
    pallas_call x1, Pallas kernels, on_device(): pl.pallas_call(functools.partial(kernel, nd, nz, tokens_all), out_shape=(...  25.3 us
    unnamed x2, local copies, waits for them, and re-layouts  1.19 us

profile of v3, /device:TPU:0, one launch (start us, length us, event | category | flops | bytes accessed | tf_op | source)
XLA Modules:
  0.0 27.1 jit_solution(16078942946842357089)
XLA Ops:
  0.6 25.3 %shard_map.50 = (f32[4,8,512]{2,1,0:T(8,128)S(1)}, f32[2,4]{1,0:T(2,128)S(1)}) custom-call(bf16[4,256,4096]{2,1,0:T(8,128)(2,1)} %x_hbm.1, bf16[4,8,4096]{2,1,0:T(8,128)(2,1)} %w_hbm.1, s32[4,2,256]{2,1,0:T(2,128)} %bitcast.3), custom_call_target="tpu_custom_call" | custom-call | tf_op jit(solution)/shard_map/pallas_call | solution.py:209
  25.9 0.6 %copy.7 = f32[4,8,512]{2,1,0:T(8,128)} copy(f32[4,8,512]{2,1,0:T(8,128)S(1)} %get-tuple-element.6) | data formatting | bytes 131072
  26.5 0.6 %copy.8 = f32[4,2]{0,1:T(2,128)} copy(f32[4,2]{0,1:T(2,128)S(1)} %bitcast.2) | data formatting | bytes 64
